TPU v7x, 32 devices: a whole 2x2x4 slice. The times are simulated.
32 devices in a mesh: band: 8 (over z, x), patch: 4 (over y, core).
Axes of the slice: x: 2, y: 2, z: 4, core: 2. Of those that a mesh axis runs over, the one named last changes fastest.
Arguments:
- latents: bfloat16 [8, 10240, 512], P('band', 'patch'), may hold values from -6 to 6
- owners: int32 [16], replicated, may hold values from 0 to 3, as said below
- block_rows: int32 [16, 128], replicated, may hold values from 0 to 2559
- interp_weights: bfloat16 [16, 1024, 128], P('band', 'patch'), may hold values from -0.5 to 0.5
- w_first: bfloat16 [8, 512, 512], P('band'), may hold values from -0.25 to 0.25
- b_first: float32 [8, 512], P('band'), may hold values from -3 to 3
- w_second: bfloat16 [8, 512, 512], P('band'), may hold values from -0.25 to 0.25
- b_second: float32 [8, 512], P('band'), may hold values from -4 to 4
- gain: float32 [8, 512], P('band'), may hold values from 0.1 to 1.9
- w_out: bfloat16 [8, 12, 512], P('band'), may hold values from -0.25 to 0.25
- b_out: float32 [8, 12], P('band'), may hold values from -4 to 4
Outputs:
- grid_fields: float32 [8, 12, 16384], P('band', None, 'patch')
Inputs may be any that keep to these rules, and one draw needn't show every extreme that they name: `owners`: no patch owns more than 8 tiles, and one patch owns exactly 8.
All inputs are finite; a program needn't handle non-finite values.
Results may differ from a plain program's by a relative error of at most 0.003.
Values may be sent and summed in bfloat16 or wider, within the bound.
A program may use at most 64 MiB of HBM per device.

v0:
```python
import jax
import jax.numpy as jnp
from jax import lax
from jax.sharding import PartitionSpec as P


def decode_rows(interp, w_first, b_first, w_second, b_second, gain, w_out, b_out):
    hidden = jax.nn.silu(
        jnp.dot(interp, w_first, preferred_element_type=jnp.float32) + b_first
    ).astype(jnp.bfloat16)
    second = jnp.dot(hidden, w_second, preferred_element_type=jnp.float32) + b_second
    mean_value = jnp.mean(second, axis=-1, keepdims=True)
    centred = second - mean_value
    variance = jnp.mean(centred * centred, axis=-1, keepdims=True)
    normed = (centred * lax.rsqrt(variance + 1e-05) * gain).astype(jnp.bfloat16)
    result = lax.dot_general(
        w_out, normed, (((1,), (1,)), ((), ())), preferred_element_type=jnp.float32
    )
    return result + b_out[:, None]


def body(
    latents,
    owners,
    block_rows,
    interp_weights,
    w_first,
    b_first,
    w_second,
    b_second,
    gain,
    w_out,
    b_out,
):
    tile_count = owners.shape[0]
    cell_count = interp_weights.shape[1]
    channels = w_out.shape[1]
    local_latents = latents[0]
    width = local_latents.shape[1]
    weights_all = lax.all_gather(interp_weights, "band", axis=0, tiled=True)

    def decode_tile(tile_index, block):
        tile_weights = lax.dynamic_index_in_dim(weights_all, tile_index, 0, keepdims=False)
        interp = jnp.dot(tile_weights, block, preferred_element_type=jnp.float32).astype(
            jnp.bfloat16
        )
        return decode_rows(
            interp, w_first[0], b_first[0], w_second[0], b_second[0], gain[0], w_out[0], b_out[0]
        )

    empty = jnp.zeros((channels, tile_count, cell_count), jnp.float32)
    my_index = lax.axis_index("patch")
    own_tiles = jnp.take(local_latents, block_rows.reshape(-1), axis=0).reshape(
        tile_count, -1, width
    )
    mine = (owners == my_index)[:, None, None]
    filled = jnp.where(mine, own_tiles.astype(jnp.float32), jnp.float32(0.0))
    all_blocks = lax.psum(filled.astype(jnp.bfloat16), "patch")

    def visit_summed(turn_index, buffer):
        tile_index = turn_index % tile_count
        block = lax.dynamic_index_in_dim(all_blocks, tile_index, 0, keepdims=False)
        result = decode_tile(tile_index, block)
        return lax.dynamic_update_index_in_dim(buffer, result, tile_index, 1)

    decoded = lax.fori_loop(0, tile_count, visit_summed, empty)
    regrid = lax.all_to_all(decoded, "patch", split_axis=1, concat_axis=2, tiled=True)
    return regrid.reshape(channels, -1)[None]


def solution(mesh):
    return jax.shard_map(
        body,
        mesh=mesh,
        in_specs=(
            P("band", "patch", None),
            P(),
            P(),
            P("band", "patch", None),
            P("band", None, None),
            P("band", None),
            P("band", None, None),
            P("band", None),
            P("band", None),
            P("band", None, None),
            P("band", None),
        ),
        out_specs=P("band", None, "patch"),
        check_vma=False,
    )
```

profile of v0, /device:TPU:0, one launch (start us, length us, event | category | flops | bytes accessed | tf_op | source)
XLA Modules:
  0.0 144.4 jit_solution(14935995324864705536)
XLA Ops:
  7.4 0.9 compare_and_fusion
  8.2 0.7 compare_select_fusion
  9.1 9.2 %gather_fusion = bf16[2048,512]{1,0:T(8,128)(2,1)} fusion(bf16[2560,512]{1,0:T(8,128)(2,1)S(1)} %bitcast.62, s32[2048]{0:T(1024)S(1)} %broadcast_clamp_fusion), kind=kCustom, calls=%fused_computation | custom fusion | bytes 4202496 | tf_op jit(solution)/shard_map/jit(_take)/gather | solution.py:53
  18.3 2.9 %select_convert_fusion = bf16[16,128,512]{2,1,0:T(8,128)(2,1)} fusion(bf16[16,128,512]{2,1,0:T(8,128)(2,1)} %bitcast.63, pred[16]{0:T(512)(128)(4,1)S(1)} %broadcast_compare_fusion, pred[16,128]{1,0:T(8,128)(4,1)S(1)} %compare_and_fusion), kind=kLoop, calls=%fused_computation.23 | loop fusion | flops 4194304 | bytes 4196368 | tf_op jit(solution)/shard_map/convert_element_type | solution.py:58
  21.3 0.5 all-gather.2.cloned.1.call-update
  21.9 53.7 %all-reduce.2.cloned.1.call-done = bf16[16,128,512]{2,1,0:T(8,128)(2,1)} async-done(((bf16[16,128,512]{2,1,0:T(8,128)(2,1)}), bf16[16,128,512]{2,1,0:T(8,128)(2,1)}) %all-reduce.2.cloned.1.call-update) | async-done | bytes 2097168 | tf_op jit(solution)/shard_map/psum | solution.py:58
  75.6 0.7 broadcast_in_dim.43
  76.3 50.2 %while.15 = (s32[]{:T(128)}, f32[12,16,256]{2,0,1:T(8,128)}, bf16[16,256,128]{2,1,0:T(8,128)(2,1)}, bf16[16,128,512]{2,1,0:T(8,128)(2,1)}, bf16[1,512,512]{2,1,0...) while((s32[]{:T(128)}, f32[12,16,256]{2,0,1:T(8,128)}, ...), condition=%wide.region_4.5_spmd, body=%wide.region_1.4_spmd.sunk | while | flops 307236096 | bytes 3387677 | solution.py:66
  76.3 1.7 %multiply_convert_fusion.6 = bf16[256,512]{1,0:T(8,128)(2,1)S(1)} fusion(bf16[1,512,512]{2,1,0:T(8,128)(2,1)} %get-tuple-element.400, f32[512]{0:T(512)S(1)} %bitcast.71, bf16[16,128,512]{2,1,0:T(8,128)(2,1)} %get-tuple-element.399, s32[]{:T(128)S(6)} %select_n.74, bf16[16,256,128]{2,1,0:T(8,128)(2,1)} %get-tuple-element.398), kind=kOutput, calls=%fused_computation.11.clone.1 | convolution fusion | flops 168689664 | bytes 986112 | tf_op jit(solution)/shard_map/while/body/eval_jaxpr/dot_general | solution.py:9
  78.0 0.4 fusion.34
  78.6 0.9 fusion.35
  79.5 1.6 %multiply_convert_fusion.6 = bf16[256,512]{1,0:T(8,128)(2,1)S(1)} fusion(bf16[1,512,512]{2,1,0:T(8,128)(2,1)} %get-tuple-element.400, f32[512]{0:T(512)S(1)} %bitcast.71, bf16[16,128,512]{2,1,0:T(8,128)(2,1)} %get-tuple-element.399, s32[]{:T(128)S(6)} %select_n.74, bf16[16,256,128]{2,1,0:T(8,128)(2,1)} %get-tuple-element.398), kind=kOutput, calls=%fused_computation.11.clone.1 | convolution fusion | flops 168689664 | bytes 986112 | tf_op jit(solution)/shard_map/while/body/eval_jaxpr/dot_general | solution.py:9
  81.1 0.4 fusion.34
  81.7 0.9 fusion.35
  82.6 1.6 %multiply_convert_fusion.6 = bf16[256,512]{1,0:T(8,128)(2,1)S(1)} fusion(bf16[1,512,512]{2,1,0:T(8,128)(2,1)} %get-tuple-element.400, f32[512]{0:T(512)S(1)} %bitcast.71, bf16[16,128,512]{2,1,0:T(8,128)(2,1)} %get-tuple-element.399, s32[]{:T(128)S(6)} %select_n.74, bf16[16,256,128]{2,1,0:T(8,128)(2,1)} %get-tuple-element.398), kind=kOutput, calls=%fused_computation.11.clone.1 | convolution fusion | flops 168689664 | bytes 986112 | tf_op jit(solution)/shard_map/while/body/eval_jaxpr/dot_general | solution.py:9
  84.2 0.4 fusion.34
  84.9 0.9 fusion.35
  85.7 1.6 %multiply_convert_fusion.6 = bf16[256,512]{1,0:T(8,128)(2,1)S(1)} fusion(bf16[1,512,512]{2,1,0:T(8,128)(2,1)} %get-tuple-element.400, f32[512]{0:T(512)S(1)} %bitcast.71, bf16[16,128,512]{2,1,0:T(8,128)(2,1)} %get-tuple-element.399, s32[]{:T(128)S(6)} %select_n.74, bf16[16,256,128]{2,1,0:T(8,128)(2,1)} %get-tuple-element.398), kind=kOutput, calls=%fused_computation.11.clone.1 | convolution fusion | flops 168689664 | bytes 986112 | tf_op jit(solution)/shard_map/while/body/eval_jaxpr/dot_general | solution.py:9
  88.0 0.9 fusion.35
  88.9 1.6 %multiply_convert_fusion.6 = bf16[256,512]{1,0:T(8,128)(2,1)S(1)} fusion(bf16[1,512,512]{2,1,0:T(8,128)(2,1)} %get-tuple-element.400, f32[512]{0:T(512)S(1)} %bitcast.71, bf16[16,128,512]{2,1,0:T(8,128)(2,1)} %get-tuple-element.399, s32[]{:T(128)S(6)} %select_n.74, bf16[16,256,128]{2,1,0:T(8,128)(2,1)} %get-tuple-element.398), kind=kOutput, calls=%fused_computation.11.clone.1 | convolution fusion | flops 168689664 | bytes 986112 | tf_op jit(solution)/shard_map/while/body/eval_jaxpr/dot_general | solution.py:9
  91.1 0.9 fusion.35
  92.0 1.6 %multiply_convert_fusion.6 = bf16[256,512]{1,0:T(8,128)(2,1)S(1)} fusion(bf16[1,512,512]{2,1,0:T(8,128)(2,1)} %get-tuple-element.400, f32[512]{0:T(512)S(1)} %bitcast.71, bf16[16,128,512]{2,1,0:T(8,128)(2,1)} %get-tuple-element.399, s32[]{:T(128)S(6)} %select_n.74, bf16[16,256,128]{2,1,0:T(8,128)(2,1)} %get-tuple-element.398), kind=kOutput, calls=%fused_computation.11.clone.1 | convolution fusion | flops 168689664 | bytes 986112 | tf_op jit(solution)/shard_map/while/body/eval_jaxpr/dot_general | solution.py:9
  93.7 0.4 fusion.34
  94.3 0.9 fusion.35
  95.1 1.6 %multiply_convert_fusion.6 = bf16[256,512]{1,0:T(8,128)(2,1)S(1)} fusion(bf16[1,512,512]{2,1,0:T(8,128)(2,1)} %get-tuple-element.400, f32[512]{0:T(512)S(1)} %bitcast.71, bf16[16,128,512]{2,1,0:T(8,128)(2,1)} %get-tuple-element.399, s32[]{:T(128)S(6)} %select_n.74, bf16[16,256,128]{2,1,0:T(8,128)(2,1)} %get-tuple-element.398), kind=kOutput, calls=%fused_computation.11.clone.1 | convolution fusion | flops 168689664 | bytes 986112 | tf_op jit(solution)/shard_map/while/body/eval_jaxpr/dot_general | solution.py:9
  96.8 0.4 fusion.34
  97.4 0.9 fusion.35
  98.3 1.6 %multiply_convert_fusion.6 = bf16[256,512]{1,0:T(8,128)(2,1)S(1)} fusion(bf16[1,512,512]{2,1,0:T(8,128)(2,1)} %get-tuple-element.400, f32[512]{0:T(512)S(1)} %bitcast.71, bf16[16,128,512]{2,1,0:T(8,128)(2,1)} %get-tuple-element.399, s32[]{:T(128)S(6)} %select_n.74, bf16[16,256,128]{2,1,0:T(8,128)(2,1)} %get-tuple-element.398), kind=kOutput, calls=%fused_computation.11.clone.1 | convolution fusion | flops 168689664 | bytes 986112 | tf_op jit(solution)/shard_map/while/body/eval_jaxpr/dot_general | solution.py:9
  100.6 0.9 fusion.35
  101.4 1.6 %multiply_convert_fusion.6 = bf16[256,512]{1,0:T(8,128)(2,1)S(1)} fusion(bf16[1,512,512]{2,1,0:T(8,128)(2,1)} %get-tuple-element.400, f32[512]{0:T(512)S(1)} %bitcast.71, bf16[16,128,512]{2,1,0:T(8,128)(2,1)} %get-tuple-element.399, s32[]{:T(128)S(6)} %select_n.74, bf16[16,256,128]{2,1,0:T(8,128)(2,1)} %get-tuple-element.398), kind=kOutput, calls=%fused_computation.11.clone.1 | convolution fusion | flops 168689664 | bytes 986112 | tf_op jit(solution)/shard_map/while/body/eval_jaxpr/dot_general | solution.py:9
  103.1 0.4 fusion.34
  103.7 0.9 fusion.35
  104.6 1.6 %multiply_convert_fusion.6 = bf16[256,512]{1,0:T(8,128)(2,1)S(1)} fusion(bf16[1,512,512]{2,1,0:T(8,128)(2,1)} %get-tuple-element.400, f32[512]{0:T(512)S(1)} %bitcast.71, bf16[16,128,512]{2,1,0:T(8,128)(2,1)} %get-tuple-element.399, s32[]{:T(128)S(6)} %select_n.74, bf16[16,256,128]{2,1,0:T(8,128)(2,1)} %get-tuple-element.398), kind=kOutput, calls=%fused_computation.11.clone.1 | convolution fusion | flops 168689664 | bytes 986112 | tf_op jit(solution)/shard_map/while/body/eval_jaxpr/dot_general | solution.py:9
  106.8 0.9 fusion.35
  107.7 1.6 %multiply_convert_fusion.6 = bf16[256,512]{1,0:T(8,128)(2,1)S(1)} fusion(bf16[1,512,512]{2,1,0:T(8,128)(2,1)} %get-tuple-element.400, f32[512]{0:T(512)S(1)} %bitcast.71, bf16[16,128,512]{2,1,0:T(8,128)(2,1)} %get-tuple-element.399, s32[]{:T(128)S(6)} %select_n.74, bf16[16,256,128]{2,1,0:T(8,128)(2,1)} %get-tuple-element.398), kind=kOutput, calls=%fused_computation.11.clone.1 | convolution fusion | flops 168689664 | bytes 986112 | tf_op jit(solution)/shard_map/while/body/eval_jaxpr/dot_general | solution.py:9
  110.0 0.9 fusion.35
  110.8 1.6 %multiply_convert_fusion.6 = bf16[256,512]{1,0:T(8,128)(2,1)S(1)} fusion(bf16[1,512,512]{2,1,0:T(8,128)(2,1)} %get-tuple-element.400, f32[512]{0:T(512)S(1)} %bitcast.71, bf16[16,128,512]{2,1,0:T(8,128)(2,1)} %get-tuple-element.399, s32[]{:T(128)S(6)} %select_n.74, bf16[16,256,128]{2,1,0:T(8,128)(2,1)} %get-tuple-element.398), kind=kOutput, calls=%fused_computation.11.clone.1 | convolution fusion | flops 168689664 | bytes 986112 | tf_op jit(solution)/shard_map/while/body/eval_jaxpr/dot_general | solution.py:9
  113.1 0.9 fusion.35
  114.0 1.7 %multiply_convert_fusion.6 = bf16[256,512]{1,0:T(8,128)(2,1)S(1)} fusion(bf16[1,512,512]{2,1,0:T(8,128)(2,1)} %get-tuple-element.400, f32[512]{0:T(512)S(1)} %bitcast.71, bf16[16,128,512]{2,1,0:T(8,128)(2,1)} %get-tuple-element.399, s32[]{:T(128)S(6)} %select_n.74, bf16[16,256,128]{2,1,0:T(8,128)(2,1)} %get-tuple-element.398), kind=kOutput, calls=%fused_computation.11.clone.1 | convolution fusion | flops 168689664 | bytes 986112 | tf_op jit(solution)/shard_map/while/body/eval_jaxpr/dot_general | solution.py:9
  116.2 0.9 fusion.35
  117.1 1.6 %multiply_convert_fusion.6 = bf16[256,512]{1,0:T(8,128)(2,1)S(1)} fusion(bf16[1,512,512]{2,1,0:T(8,128)(2,1)} %get-tuple-element.400, f32[512]{0:T(512)S(1)} %bitcast.71, bf16[16,128,512]{2,1,0:T(8,128)(2,1)} %get-tuple-element.399, s32[]{:T(128)S(6)} %select_n.74, bf16[16,256,128]{2,1,0:T(8,128)(2,1)} %get-tuple-element.398), kind=kOutput, calls=%fused_computation.11.clone.1 | convolution fusion | flops 168689664 | bytes 986112 | tf_op jit(solution)/shard_map/while/body/eval_jaxpr/dot_general | solution.py:9
  119.4 0.9 fusion.35
  120.2 1.6 %multiply_convert_fusion.6 = bf16[256,512]{1,0:T(8,128)(2,1)S(1)} fusion(bf16[1,512,512]{2,1,0:T(8,128)(2,1)} %get-tuple-element.400, f32[512]{0:T(512)S(1)} %bitcast.71, bf16[16,128,512]{2,1,0:T(8,128)(2,1)} %get-tuple-element.399, s32[]{:T(128)S(6)} %select_n.74, bf16[16,256,128]{2,1,0:T(8,128)(2,1)} %get-tuple-element.398), kind=kOutput, calls=%fused_computation.11.clone.1 | convolution fusion | flops 168689664 | bytes 986112 | tf_op jit(solution)/shard_map/while/body/eval_jaxpr/dot_general | solution.py:9
  122.5 0.9 fusion.35
  123.4 1.6 %multiply_convert_fusion.6 = bf16[256,512]{1,0:T(8,128)(2,1)S(1)} fusion(bf16[1,512,512]{2,1,0:T(8,128)(2,1)} %get-tuple-element.400, f32[512]{0:T(512)S(1)} %bitcast.71, bf16[16,128,512]{2,1,0:T(8,128)(2,1)} %get-tuple-element.399, s32[]{:T(128)S(6)} %select_n.74, bf16[16,256,128]{2,1,0:T(8,128)(2,1)} %get-tuple-element.398), kind=kOutput, calls=%fused_computation.11.clone.1 | convolution fusion | flops 168689664 | bytes 986112 | tf_op jit(solution)/shard_map/while/body/eval_jaxpr/dot_general | solution.py:9
  125.6 0.9 fusion.35
  126.5 9.4 %all_to_all.15 = f32[12,16,256]{2,0,1:T(8,128)S(1)} all-to-all(f32[12,16,256]{2,0,1:T(8,128)} %get-tuple-element.270), channel_id=1, replica_groups=mesh['band'=8,'patch'=4] {'patch'}, dimensions={1} | all-to-all | bytes 393216 | tf_op jit(solution)/shard_map/all_to_all | solution.py:67
  136.0 0.9 broadcast_in_dim_reshape.3
  (81 shorter events, 7.7 us)
Async XLA Ops:
  7.4 1.8 %copy-start = (bf16[1,2560,512]{2,1,0:T(8,128)(2,1)S(1)}, bf16[1,2560,512]{2,1,0:T(8,128)(2,1)}, u32[]{:S(2)}) copy-start(bf16[1,2560,512]{2,1,0:T(8,128)(2,1)} %param.13) | copy-start | bytes 7864324
  7.4 68.2 %all-reduce.2.cloned.1.call-start = ((), (), s32[]{:S(2)}) async-start(), calls=%async_computation.2 | async-start | bytes 4194304 | tf_op jit(solution)/shard_map/psum | solution.py:58
  9.1 9.2 %copy-start.7 = (s32[16]{0:T(128)S(1)}, s32[16]{0:T(128)}, u32[]{:S(2)}) copy-start(s32[16]{0:T(128)} %param.14) | copy-start | bytes 196
  21.2 55.1 %copy-start.1 = (bf16[1,512,512]{2,1,0:T(8,128)(2,1)S(1)}, bf16[1,512,512]{2,1,0:T(8,128)(2,1)}, u32[]{:S(2)}) copy-start(bf16[1,512,512]{2,1,0:T(8,128)(2,1)} %param.19) | copy-start | bytes 1572868
  21.2 55.1 %copy-start.2 = (bf16[1,12,512]{2,1,0:T(8,128)(2,1)S(1)}, bf16[1,12,512]{2,1,0:T(8,128)(2,1)}, u32[]{:S(2)}) copy-start(bf16[1,12,512]{2,1,0:T(8,128)(2,1)} %param.22) | copy-start | bytes 36868
  21.2 55.1 %copy-start.3 = (f32[1,512]{1,0:T(1,128)S(1)}, f32[1,512]{1,0:T(1,128)}, u32[]{:S(2)}) copy-start(f32[1,512]{1,0:T(1,128)} %param.20) | copy-start | bytes 6148
  21.2 55.1 %copy-start.4 = (f32[1,512]{1,0:T(1,128)S(1)}, f32[1,512]{1,0:T(1,128)}, u32[]{:S(2)}) copy-start(f32[1,512]{1,0:T(1,128)} %param.21) | copy-start | bytes 6148
  21.2 55.1 %copy-start.5 = (f32[1,12]{1,0:T(1,128)S(1)}, f32[1,12]{1,0:T(1,128)}, u32[]{:S(2)}) copy-start(f32[1,12]{1,0:T(1,128)} %param.23) | copy-start | bytes 148
  21.2 55.1 %copy-start.6 = (f32[1,512]{1,0:T(1,128)S(1)}, f32[1,512]{1,0:T(1,128)}, u32[]{:S(2)}) copy-start(f32[1,512]{1,0:T(1,128)} %param.18) | copy-start | bytes 6148
  21.3 54.3 %all-gather.2.cloned.1.call-start = ((), (), s32[]{:S(2)}) async-start(), calls=%async_computation.1 | async-start | bytes 1179648 | tf_op jit(solution)/shard_map/all_gather | solution.py:40
Sparse Core Ops, SparseCore 0:
  21.4 54.1 all-reduce.1
Sparse Core Ops, SparseCore 1:
  23.9 43.0 all-gather.1
where the time goes:
time: 145 us; the launch traced here: 144 us
  waiting for transfers between devices  54.2 us (37%)
  matrix products  46.4 us (32%)
  between operations  14.9 us (10%)
  local copies, waits for them, and re-layouts  11.2 us (8%)
  blocking collectives  9.38 us (6%)
  other arithmetic  7.95 us (5%)
    psum x1, waiting for transfers between devices, body(): all_blocks = lax.psum(filled.astype(jnp.bfloat16), 'patch')  53.7 us
    dot_general x16, matrix products, decode_rows(): jnp.dot(interp, w_first, preferred_element_type=jnp.float32) + b_first  26.3 us
    dot_general x16, matrix products, decode_rows(): lax.dot_general(w_out, normed, (((1,), (1,)), ((), ())), preferred_elemen...  13.9 us
    all_to_all x1, blocking collectives, body(): lax.all_to_all(decoded, 'patch', split_axis=1, concat_axis=2, tiled=True)  9.38 us
    gather x1, local copies, waits for them, and re-layouts, body(): jnp.take(local_latents, block_rows.reshape(-1), axis=0)  9.18 us
    dot_general x16, matrix products, decode_rows(): jnp.dot(hidden, w_second, preferred_element_type=jnp.float32) + b_second  6.16 us
    reduce_sum x16, other arithmetic, decode_rows(): variance = jnp.mean(centred * centred, axis=-1, keepdims=True)  3.28 us
    convert_element_type x1, other arithmetic, body(): all_blocks = lax.psum(filled.astype(jnp.bfloat16), 'patch')  2.9 us
  transfers between devices with their start and end apart: 2, of which 1 were waited for; matrix products, arithmetic and copies ran while one was open for 0% of the time, Pallas kernels for 0%

commit v1 on v0

--- a/solution.py
+++ b/solution.py
@@ -55,7 +55,9 @@
     )
     mine = (owners == my_index)[:, None, None]
     filled = jnp.where(mine, own_tiles.astype(jnp.float32), jnp.float32(0.0))
-    all_blocks = lax.psum(filled.astype(jnp.bfloat16), "patch")
+    own = filled.astype(jnp.bfloat16)
+    parts = lax.all_gather(own, "patch", axis=0, tiled=False)
+    all_blocks = parts.sum(axis=0)
 
     def visit_summed(turn_index, buffer):
         tile_index = turn_index % tile_count

time: 145 us -> 193 us (1.33)
  waiting for transfers between devices: 54.2 us -> 96.6 us
  other arithmetic: 7.95 us -> 14.9 us
    all_gather x0 -> x1, waiting for transfers between devices: none -> 60.3 us  [body(): parts = lax.all_gather(own, 'patch', axis=0, tiled=False)]
    psum x1 -> x0, waiting for transfers between devices: 53.7 us -> none  [body(): all_blocks = lax.psum(filled.astype(jnp.bfloat16), 'patch')]
    all_gather x1, waiting for transfers between devices: 0.01 us -> 35.5 us  [body(): weights_all = lax.all_gather(interp_weights, 'band', axis=0, tiled=True)]
    reduce_sum x0 -> x1, other arithmetic: none -> 6.9 us  [body(): all_blocks = parts.sum(axis=0)]
  transfers between devices with their start and end apart: 2 -> 2, of which waited for: 1 -> 2; matrix products, arithmetic and copies ran while one was open for 0% -> 4% of each run, Pallas kernels for 0% -> 0%
where the time goes in v1:
time: 193 us; the launch traced here: 192 us
  waiting for transfers between devices  96.6 us (50%)
  matrix products  46.4 us (24%)
  other arithmetic  14.9 us (8%)
  between operations  13.5 us (7%)
  local copies, waits for them, and re-layouts  11.2 us (6%)
  blocking collectives  9.38 us (5%)
    all_gather x1, waiting for transfers between devices, body(): parts = lax.all_gather(own, 'patch', axis=0, tiled=False)  60.3 us
    all_gather x1, waiting for transfers between devices, body(): weights_all = lax.all_gather(interp_weights, 'band', axis=0, tiled=True)  35.5 us
    dot_general x16, matrix products, decode_rows(): jnp.dot(interp, w_first, preferred_element_type=jnp.float32) + b_first  26.4 us
    dot_general x16, matrix products, decode_rows(): lax.dot_general(w_out, normed, (((1,), (1,)), ((), ())), preferred_elemen...  13.9 us
    all_to_all x1, blocking collectives, body(): lax.all_to_all(decoded, 'patch', split_axis=1, concat_axis=2, tiled=True)  9.38 us
    gather x1, local copies, waits for them, and re-layouts, body(): jnp.take(local_latents, block_rows.reshape(-1), axis=0)  9.18 us
    reduce_sum x1, other arithmetic, body(): all_blocks = parts.sum(axis=0)  6.9 us
    dot_general x16, matrix products, decode_rows(): jnp.dot(hidden, w_second, preferred_element_type=jnp.float32) + b_second  6.12 us
  transfers between devices with their start and end apart: 2, of which 2 were waited for; matrix products, arithmetic and copies ran while one was open for 4% of the time, Pallas kernels for 0%

profile of v1, /device:TPU:0, one launch (start us, length us, event | category | flops | bytes accessed | tf_op | source)
XLA Modules:
  0.0 192.2 jit_solution(4998509393439330468)
XLA Ops:
  6.5 0.9 compare_and_fusion
  7.4 0.7 compare_select_fusion
  8.3 9.2 %gather_fusion = bf16[2048,512]{1,0:T(8,128)(2,1)} fusion(bf16[2560,512]{1,0:T(8,128)(2,1)S(1)} %bitcast.62, s32[2048]{0:T(1024)S(1)} %broadcast_clamp_fusion), kind=kCustom, calls=%fused_computation | custom fusion | bytes 4202496 | tf_op jit(solution)/shard_map/jit(_take)/gather | solution.py:53
  17.5 2.9 %select_convert_fusion = bf16[1,16,128,512]{3,2,1,0:T(8,128)(2,1)} fusion(bf16[1,16,128,512]{3,2,1,0:T(8,128)(2,1)} %bitcast.63, pred[16]{0:T(512)(128)(4,1)S(1)} %broadcast_compare_fusion, pred[16,128]{1,0:T(8,128)(4,1)S(1)} %compare_and_fusion), kind=kLoop, calls=%fused_computation.23 | loop fusion | flops 4194304 | bytes 4196368 | tf_op jit(solution)/shard_map/convert_element_type | solution.py:58
  20.5 0.7 all-gather.3.cloned.1.call-update
  21.3 60.3 %all-gather.5.cloned.1.call-done = bf16[4,16,128,512]{3,2,1,0:T(8,128)(2,1)} async-done(((bf16[1,16,128,512]{3,2,1,0:T(8,128)(2,1)}), bf16[4,16,128,512]{3,2,1,0:T(8,128)(2,1)}) %all-gather.5.cloned.1.call-update) | async-done | bytes 8388624 | tf_op jit(solution)/shard_map/all_gather | solution.py:59
  81.6 6.9 %reduce_sum.44 = bf16[16,128,512]{2,1,0:T(8,128)(2,1)} reduce(bf16[4,16,128,512]{3,2,1,0:T(8,128)(2,1)} %all-gather.5.cloned.1.call-done, bf16[]{:T(256)} %constant.124.clone.1), dimensions={0}, to_apply=%region_0.1 | reduce | flops 3145728 | bytes 10485762 | tf_op jit(solution)/shard_map/reduce_sum | solution.py:60
  88.5 35.5 %all-gather.3.cloned.1.call-done = bf16[16,256,128]{2,1,0:T(8,128)(2,1)} async-done(((bf16[2,256,128]{2,1,0:T(8,128)(2,1)}), bf16[16,256,128]{2,1,0:T(8,128)(2,1)}) %all-gather.3.cloned.1.call-update) | async-done | bytes 1048592 | tf_op jit(solution)/shard_map/all_gather | solution.py:40
  124.0 0.7 broadcast_in_dim.43
  124.8 50.2 %while.15 = (s32[]{:T(128)}, f32[12,16,256]{2,0,1:T(8,128)}, bf16[16,256,128]{2,1,0:T(8,128)(2,1)}, bf16[16,128,512]{2,1,0:T(8,128)(2,1)}, bf16[1,512,512]{2,1,0...) while((s32[]{:T(128)}, f32[12,16,256]{2,0,1:T(8,128)}, ...), condition=%wide.region_4.5_spmd, body=%wide.region_1.4_spmd.sunk | while | flops 307236096 | bytes 3387677 | solution.py:68
  124.8 1.7 multiply_convert_fusion.6
  127.0 0.9 fusion.35
  127.9 1.6 multiply_convert_fusion.6
  130.2 0.9 fusion.35
  131.0 1.6 multiply_convert_fusion.6
  132.7 0.4 fusion.34
  133.3 0.9 fusion.35
  134.2 1.6 multiply_convert_fusion.6
  136.4 0.9 fusion.35
  137.3 1.7 multiply_convert_fusion.6
  139.6 0.9 fusion.35
  140.5 1.7 multiply_convert_fusion.6
  142.1 0.4 fusion.34
  142.7 0.9 fusion.35
  143.6 1.6 multiply_convert_fusion.6
  145.9 0.9 fusion.35
  146.7 1.6 multiply_convert_fusion.6
  149.0 0.9 fusion.35
  149.9 1.6 multiply_convert_fusion.6
  152.1 0.9 fusion.35
  153.0 1.7 multiply_convert_fusion.6
  155.3 0.9 fusion.35
  156.1 1.6 multiply_convert_fusion.6
  158.4 0.9 fusion.35
  159.3 1.7 multiply_convert_fusion.6
  161.5 0.9 fusion.35
  162.4 1.6 multiply_convert_fusion.6
  164.7 0.9 fusion.35
  165.5 1.7 multiply_convert_fusion.6
  167.2 0.4 fusion.34
  167.8 0.9 fusion.35
  168.7 1.6 multiply_convert_fusion.6
  170.9 0.9 fusion.35
  171.8 1.6 multiply_convert_fusion.6
  173.5 0.4 fusion.34
  174.1 0.9 fusion.35
  175.0 9.4 %all_to_all.15 = f32[12,16,256]{2,0,1:T(8,128)S(1)} all-to-all(f32[12,16,256]{2,0,1:T(8,128)} %get-tuple-element.270), channel_id=1, replica_groups=mesh['band'=8,'patch'=4] {'patch'}, dimensions={1} | all-to-all | bytes 393216 | tf_op jit(solution)/shard_map/all_to_all | solution.py:69
  184.5 0.9 broadcast_in_dim_reshape.3
  (82 shorter events, 8.5 us)
Async XLA Ops:
  6.5 1.8 copy-start
  6.5 75.0 %all-gather.5.cloned.1.call-start = ((), (), s32[]{:S(2)}) async-start(), calls=%async_computation.2 | async-start | bytes 10485760 | tf_op jit(solution)/shard_map/all_gather | solution.py:59
  8.3 9.2 %copy-start.7 = (s32[16]{0:T(128)S(1)}, s32[16]{0:T(128)}, u32[]{:S(2)}) copy-start(s32[16]{0:T(128)} %param.14) | copy-start | bytes 196
  20.4 103.6 %all-gather.3.cloned.1.call-start = ((), (), s32[]{:S(2)}) async-start(), calls=%async_computation.1 | async-start | bytes 1179648 | tf_op jit(solution)/shard_map/all_gather | solution.py:40
  21.2 103.5 %copy-start.1 = (bf16[1,512,512]{2,1,0:T(8,128)(2,1)S(1)}, bf16[1,512,512]{2,1,0:T(8,128)(2,1)}, u32[]{:S(2)}) copy-start(bf16[1,512,512]{2,1,0:T(8,128)(2,1)} %param.19) | copy-start | bytes 1572868
  21.2 103.5 %copy-start.2 = (bf16[1,12,512]{2,1,0:T(8,128)(2,1)S(1)}, bf16[1,12,512]{2,1,0:T(8,128)(2,1)}, u32[]{:S(2)}) copy-start(bf16[1,12,512]{2,1,0:T(8,128)(2,1)} %param.22) | copy-start | bytes 36868
  21.2 103.5 %copy-start.3 = (f32[1,512]{1,0:T(1,128)S(1)}, f32[1,512]{1,0:T(1,128)}, u32[]{:S(2)}) copy-start(f32[1,512]{1,0:T(1,128)} %param.20) | copy-start | bytes 6148
  21.2 103.5 %copy-start.4 = (f32[1,512]{1,0:T(1,128)S(1)}, f32[1,512]{1,0:T(1,128)}, u32[]{:S(2)}) copy-start(f32[1,512]{1,0:T(1,128)} %param.21) | copy-start | bytes 6148
  21.2 103.5 %copy-start.5 = (f32[1,12]{1,0:T(1,128)S(1)}, f32[1,12]{1,0:T(1,128)}, u32[]{:S(2)}) copy-start(f32[1,12]{1,0:T(1,128)} %param.23) | copy-start | bytes 148
  21.2 103.5 %copy-start.6 = (f32[1,512]{1,0:T(1,128)S(1)}, f32[1,512]{1,0:T(1,128)}, u32[]{:S(2)}) copy-start(f32[1,512]{1,0:T(1,128)} %param.18) | copy-start | bytes 6148
Sparse Core Ops, SparseCore 0:
  20.6 60.9 all-gather.4
  83.7 40.2 all-gather.2
